TPU v7x, 32 devices: a whole 2x2x4 slice. The times are simulated.
32 devices in a mesh: head: 8 (over y, x, core), level: 4 (over z).
Axes of the slice: x: 2, y: 2, z: 4, core: 2. Of those that a mesh axis runs over, the one named last changes fastest.
Arguments:
- features: float32 [64, 4096], P(None, ('head', 'level')), may hold values from -6 to 6
- in_gain: float32 [4096], replicated, may hold values from 0.25 to 1.75
- in_weight: bfloat16 [4096, 4288], P(None, 'head'), may hold values from -0.09375 to 0.09375
- level_bias: float32 [8, 24], P('head'), may hold values from -4 to 252
- states: bfloat16 [64, 8, 24, 128, 128], P(None, 'head', 'level'), may hold values from -1.25 to 1.25
- positions: int32 [64], replicated, may hold values from 1 to 262143
- out_gain: float32 [1024], P('head'), may hold values from 0.25 to 1.75
- out_weight: bfloat16 [1024, 4096], P('head', 'level'), may hold values from -0.1875 to 0.1875
Outputs:
- output: float32 [64, 4096], P('head', 'level')
Inputs may be any that keep to these rules, and one draw needn't show every extreme that they name: `positions`: positions below 2 ** 18, so levels from 19 on are never occupied.
All inputs are finite; a program needn't handle non-finite values.
Results may differ from a plain program's by a relative error of at most 0.0066.
Values sent between devices are 32-bit elements; how exact they have to be, the bound alone decides.
A program may use at most 64 MiB of HBM per device.

v0:
```python
import functools

import jax
import jax.numpy as jnp
from jax import lax
from jax.experimental import pallas as pl
from jax.experimental.pallas import tpu as pltpu
from jax.sharding import PartitionSpec as P

LANES = 128
GROUP = 16


def send(src, dst, send_sem, recv_sem, target):
    return pltpu.make_async_remote_copy(
        src_ref=src,
        dst_ref=dst,
        send_sem=send_sem,
        recv_sem=recv_sem,
        device_id=target,
        device_id_type=pl.DeviceIdType.MESH,
    )


def kernel(
    heads, levels, width, dims,
    feat, gain, inw, bias, states, pos, ogain, outw, out,
    xbuf, wbuf, sbuf, owbuf, proj, abuf, bbuf, mbuf, osend, orecv, qfull, wnorm, qw, biasbuf, qsum,
    x_sem, w_sem, s_sem, ow_sem, p1_send, p1_recv, a_send, a_recv, b_send, b_recv,
    m_send, m_recv, o_send, o_recv, q_send, q_recv,
):
    key_dim, val_dim, level_total, level_here = dims
    seqs, fw = feat.shape
    flipped = fw % LANES == 0
    cols = inw.shape[0] if flipped else inw.shape[1]
    owned = seqs // levels
    out_rows = seqs // heads
    out_cols = outw.shape[1]
    me_h, me_l = lax.axis_index("head"), lax.axis_index("level")
    slot = 1 << level_total.bit_length()
    slots = LANES // slot
    packed = seqs // slots
    groups = seqs // GROUP

    x_copy = pltpu.make_async_copy(feat, xbuf.at[me_h], x_sem)
    x_copy.start()
    w_copies = []
    for h in range(heads):
        start = pl.multiple_of((h * levels + me_l) * fw, fw)
        part = inw.at[:, pl.ds(start, fw)] if flipped else inw.at[pl.ds(start, fw), :]
        w_copies.append(pltpu.make_async_copy(part, wbuf.at[h], w_sem.at[h]))
        w_copies[-1].start()
    last_group = (me_l * owned) // GROUP
    order = [lax.rem(last_group + 1 + t, groups) for t in range(groups)]

    def state_copy(g):
        rows = pl.ds(pl.multiple_of(g * GROUP, GROUP), GROUP)
        return pltpu.make_async_copy(states.at[rows], sbuf.at[rows], s_sem.at[g])

    ow_copy = pltpu.make_async_copy(outw, owbuf, ow_sem)

    barrier = pltpu.get_barrier_semaphore()
    for o in range(1, heads):
        pl.semaphore_signal(
            barrier, inc=1, device_id=(lax.rem(me_h + o, heads), me_l),
            device_id_type=pl.DeviceIdType.MESH)
    for o in range(1, levels):
        pl.semaphore_signal(
            barrier, inc=1, device_id=(me_h, lax.rem(me_l + o, levels)),
            device_id_type=pl.DeviceIdType.MESH)
    pl.semaphore_wait(barrier, heads + levels - 2)

    x_copy.wait()
    pending = []
    buddy = me_h + 1 - 2 * lax.rem(me_h, 2)
    def feature_send(block, target, index):
        c = send(xbuf.at[block], xbuf.at[block], p1_send.at[index], p1_recv.at[block], (target, me_l))
        c.start()
        pending.append(c)

    def feature_wait(block):
        send(xbuf.at[block], xbuf.at[block], p1_send.at[0], p1_recv.at[block], (buddy, me_l)).wait_recv()

    chips, core = heads // 2, lax.rem(me_h, 2)
    mirror_chip = chips - 1 - me_h // 2
    skip = lax.rem(me_h // 2 - mirror_chip + chips, chips)
    mirror = 2 * mirror_chip + core
    direct = []
    for j in range(1, chips - 1):
        near = 2 * lax.rem(mirror_chip + j + (j + chips - skip) // chips, chips)
        direct += [near + core, near + 1 - core]
    feature_send(me_h, mirror, heads - 1)
    for i, peer in enumerate(direct):
        feature_send(me_h, peer, i)
    feature_send(me_h, buddy, heads - 2)
    for c in w_copies:
        c.wait()
    acc = jnp.zeros((seqs, cols), jnp.float32)
    squares = jnp.zeros((seqs, 1), jnp.float32)
    arrivals = [me_h, buddy, mirror] + direct + [2 * mirror_chip + 1 - core]
    for i, src in enumerate(arrivals):
        if i:
            feature_wait(src)
        if i == 2:
            feature_send(mirror, buddy, heads - 3)
        x = xbuf[src]
        g = gain[pl.ds(src * levels + me_l, 1), :]
        acc += lax.dot_general(
            (x * g).astype(jnp.bfloat16), wbuf[src], (((1,), (1 if flipped else 0,)), ((), ())),
            preferred_element_type=jnp.float32)
        squares += jnp.sum(x * x, axis=1, keepdims=True)

    for g in order:
        state_copy(g).start()
    ow_copy.start()

    proj[:, :cols] = acc
    lane = lax.broadcasted_iota(jnp.int32, (seqs, LANES), 1)
    tail0 = 2 * key_dim + 2 * val_dim
    tail = jnp.where(lane < level_total, proj[:, tail0 : tail0 + LANES], 0.0)
    tail = jnp.where(lane == level_total, squares, tail)
    pack = tail[:packed]
    for c in range(1, slots):
        pack += pltpu.roll(tail[c * packed : (c + 1) * packed], slot * c, 1)
    abuf[me_l, :seqs, :] = acc[:, :key_dim]
    abuf[me_l, seqs:, :] = pack
    for o in range(1, levels):
        peer = lax.rem(me_l + o, levels)
        c = send(abuf.at[me_l], abuf.at[me_l], a_send.at[o], a_recv.at[me_l], (me_h, peer))
        c.start()
        pending.append(c)
    for o in range(1, levels):
        peer = lax.rem(me_l + o, levels)
        rows = pl.ds(pl.multiple_of(peer * owned, owned), owned)
        c = send(proj.at[rows, pl.ds(key_dim, tail0 - key_dim)], bbuf.at[me_l],
                 b_send.at[o], b_recv.at[me_l], (me_h, peer))
        c.start()
        pending.append(c)
    mine = pl.ds(pl.multiple_of(me_l * owned, owned), owned)
    bbuf[me_l] = proj[mine, key_dim:tail0]

    biasbuf[:, :level_total] = bias[...]
    row = lax.broadcasted_iota(jnp.int32, (seqs, seqs), 0)
    col = lax.broadcasted_iota(jnp.int32, (seqs, seqs), 1)
    pos_f = jnp.broadcast_to(pos[...], (seqs, seqs)).astype(jnp.float32)
    pos_col = jnp.sum(jnp.where(row == col, pos_f, 0.0), axis=1, keepdims=True).astype(jnp.int32)
    shift = jnp.clip(lane - 1, 0, 31)
    bits = jnp.bitwise_and(jnp.right_shift(jnp.broadcast_to(pos_col, lane.shape), shift), 1)
    occupied = jnp.logical_and(lane < level_total, jnp.logical_or(lane == 0, bits == 1))

    for o in range(1, levels):
        src = lax.rem(me_l + levels - o, levels)
        send(abuf.at[src], abuf.at[src], a_send.at[o], a_recv.at[src], (me_h, src)).wait_recv()
    query = abuf[0, :seqs, :]
    pack = abuf[0, seqs:, :]
    for l in range(1, levels):
        query += abuf[l, :seqs, :]
        pack += abuf[l, seqs:, :]
    parts = [pack] + [pltpu.roll(pack, LANES - slot * c, 1) for c in range(1, slots)]
    tail = jnp.concatenate(parts, axis=0)
    row_scale = lax.rsqrt(tail[:, level_total : level_total + 1] / width + 1e-06)
    query = query * row_scale
    logits = tail * row_scale + biasbuf[...]
    peak = jnp.max(jnp.where(occupied, logits, -1e30), axis=1, keepdims=True)
    weights = jnp.where(occupied, jnp.exp(logits - peak), 0.0)
    weights = weights / jnp.sum(weights, axis=1, keepdims=True)
    qfull[...] = query
    wnorm[:, :LANES] = weights
    wnorm[:, LANES:] = jnp.broadcast_to(row_scale, weights.shape)
    local = pltpu.roll(weights, lax.rem(LANES - me_l * level_here, LANES), 1)
    query_low = query.astype(jnp.bfloat16).astype(jnp.float32)
    for j in range(level_here):
        qw[:, j * key_dim : (j + 1) * key_dim] = (query_low * local[:, j : j + 1]).astype(jnp.bfloat16)

    seq_in = lax.broadcasted_iota(jnp.int32, (GROUP, val_dim), 0)
    def to_levels(rows, index):
        for o in range(1, levels):
            part = mbuf.at[me_l, rows, :]
            c = send(part, part, m_send.at[o, index], m_recv.at[me_l, index],
                     (me_h, lax.rem(me_l + o, levels)))
            c.start()
            pending.append(c)

    for t, g in enumerate(order):
        if t == groups - 1:
            for o in range(1, levels):
                src = lax.rem(me_l + levels - o, levels)
                send(bbuf.at[src], bbuf.at[src], b_send.at[o], b_recv.at[src], (me_h, src)).wait_recv()
            rest = bbuf[0]
            for l in range(1, levels):
                rest += bbuf[l]
            rest = rest * wnorm[mine, LANES : LANES + 1]
            key, value = rest[:, :key_dim], rest[:, key_dim : key_dim + val_dim]
            gate = rest[:, key_dim + val_dim :]
            own = jnp.sum(qfull[mine, :] * key, axis=1, keepdims=True) * key_dim ** (-0.5) * value
            mbuf[me_l, seqs:, :] = gate * jax.nn.sigmoid(gate)
            to_levels(pl.ds(seqs, owned), groups)
            qfull[...] = jnp.zeros(qfull.shape, jnp.float32)
            qfull[mine, :] = wnorm[mine, 0:1] * own
        state_copy(g).wait()
        base = pl.multiple_of(g * GROUP, GROUP)
        rows = pl.ds(base, GROUP)
        left = qw[rows, :]
        mixed = jnp.zeros((GROUP, val_dim), jnp.float32)
        for i in range(GROUP):
            got = jnp.dot(left, sbuf[base + i], preferred_element_type=jnp.float32)
            mixed = jnp.where(seq_in == i, got, mixed)
        if t == groups - 1:
            mixed += qfull[rows, :]
        mbuf[me_l, rows, :] = mixed
        to_levels(rows, g)
    ow_copy.wait()
    for o in range(1, levels):
        src = lax.rem(me_l + levels - o, levels)
        for index in range(groups + 1):
            rows = pl.ds(index * GROUP, GROUP if index < groups else owned)
            part = mbuf.at[src, rows, :]
            send(part, part, m_send.at[o, index], m_recv.at[src, index], (me_h, src)).wait_recv()
    gated = mbuf[0, :seqs, :]
    for l in range(1, levels):
        gated += mbuf[l, :seqs, :]
    gated = gated * jnp.concatenate([mbuf[l, seqs:, :] for l in range(levels)], axis=0)
    total_sq = jnp.sum(gated * gated, axis=1, keepdims=True)
    product = jnp.dot((gated * ogain[...]).astype(jnp.bfloat16), owbuf[...], preferred_element_type=jnp.float32)
    qsum[me_h] = jnp.sum(jnp.where(row == col, jnp.broadcast_to(total_sq, (seqs, seqs)), 0.0), axis=0, keepdims=True)
    for h in range(heads):
        osend[h] = product[h * out_rows : (h + 1) * out_rows]
    for o in range(1, heads):
        peer = lax.rem(me_h + o, heads)
        c = send(osend.at[peer], orecv.at[me_h], o_send.at[o], o_recv.at[me_h], (peer, me_l))
        c.start()
        pending.append(c)
        c = send(qsum.at[me_h], qsum.at[me_h], q_send.at[o], q_recv.at[me_h], (peer, me_l))
        c.start()
        pending.append(c)
    total = osend[me_h]
    for o in range(1, heads):
        src = lax.rem(me_h + heads - o, heads)
        send(osend.at[src], orecv.at[src], o_send.at[o], o_recv.at[src], (src, me_l)).wait_recv()
        send(qsum.at[src], qsum.at[src], q_send.at[o], q_recv.at[src], (src, me_l)).wait_recv()
        total += orecv[src]
    all_sq = qsum[0]
    for h in range(1, heads):
        all_sq += qsum[h]
    here = lax.broadcasted_iota(jnp.int32, (out_rows, seqs), 0) + me_h * out_rows
    pick = lax.broadcasted_iota(jnp.int32, (out_rows, seqs), 1) == here
    mean = jnp.sum(jnp.where(pick, jnp.broadcast_to(all_sq, pick.shape), 0.0), axis=1, keepdims=True) / (heads * val_dim)
    out[...] = total * lax.rsqrt(mean + 1e-05)
    for c in pending:
        c.wait_send()


def body(features, in_gain, in_weight, level_bias, states, positions, out_gain, out_weight):
    heads, levels = lax.axis_size("head"), lax.axis_size("level")
    seqs, fw = features.shape
    cols = in_weight.shape[1]
    _, head_here, level_here, key_dim, val_dim = states.shape
    level_total = level_bias.shape[1]
    assert head_here == 1 and key_dim == LANES and val_dim == LANES
    out_cols = out_weight.shape[1]
    flipped = fw % LANES == 0
    slots = LANES // (1 << level_total.bit_length())
    owned, out_rows = seqs // levels, seqs // heads
    f32, bf16 = jnp.float32, jnp.bfloat16
    vmem, anyspace = pl.BlockSpec(memory_space=pltpu.VMEM), pl.BlockSpec(memory_space=pl.ANY)
    dma = pltpu.SemaphoreType.DMA
    tail0 = 2 * key_dim + 2 * val_dim
    return pl.pallas_call(
        functools.partial(kernel, heads, levels, in_gain.shape[0], (key_dim, val_dim, level_total, level_here)),
        out_shape=pltpu.VMEM((out_rows, out_cols), f32),
        in_specs=[anyspace, vmem, anyspace, vmem, anyspace, vmem, vmem, anyspace],
        out_specs=vmem,
        scratch_shapes=[
            pltpu.VMEM((heads, seqs, fw), f32),
            pltpu.VMEM((heads, cols, fw) if flipped else (heads, fw, cols), bf16),
            pltpu.VMEM((seqs, level_here * key_dim, val_dim), bf16),
            pltpu.VMEM(out_weight.shape, bf16),
            pltpu.VMEM((seqs, tail0 + LANES), f32),
            pltpu.VMEM((levels, seqs + seqs // slots, key_dim), f32),
            pltpu.VMEM((levels, owned, tail0 - key_dim), f32),
            pltpu.VMEM((levels, seqs + owned, val_dim), f32),
            pltpu.VMEM((heads, out_rows, out_cols), f32),
            pltpu.VMEM((heads, out_rows, out_cols), f32),
            pltpu.VMEM((seqs, key_dim), f32),
            pltpu.VMEM((seqs, 2 * LANES), f32),
            pltpu.VMEM((seqs, level_here * key_dim), bf16),
            pltpu.VMEM((1, LANES), f32),
            pltpu.VMEM((heads, 1, seqs), f32),
            dma(()), dma((heads,)), dma((seqs // GROUP,)), dma(()),
            dma((heads,)), dma((heads,)),
            dma((levels,)), dma((levels,)), dma((levels,)), dma((levels,)),
            dma((levels, seqs // GROUP + 1)), dma((levels, seqs // GROUP + 1)),
            dma((heads,)), dma((heads,)), dma((heads,)), dma((heads,)),
        ],
        compiler_params=pltpu.CompilerParams(collective_id=0, has_side_effects=True),
    )(
        features,
        in_gain.reshape(heads * levels, fw),
        in_weight.T if flipped else in_weight,
        level_bias,
        states.reshape(seqs, level_here * key_dim, val_dim),
        positions.reshape(1, seqs),
        out_gain.reshape(1, val_dim),
        out_weight,
    )


def solution(mesh):
    in_specs = (
        P(None, ("head", "level")),
        P(),
        P(None, "head"),
        P("head", None),
        P(None, "head", "level", None, None),
        P(),
        P("head"),
        P("head", "level"),
    )
    out_specs = P("head", "level")
    return jax.shard_map(body, mesh=mesh, in_specs=in_specs, out_specs=out_specs, check_vma=False)
```

profile of v0, /device:TPU:0, one launch (start us, length us, event | category | flops | bytes accessed | tf_op | source)
XLA Modules:
  0.0 29.2 jit_solution(18120166106057866654)
XLA Ops:
  0.0 28.5 %shard_map.82 = f32[8,1024]{1,0:T(8,128)S(1)} custom-call(f32[64,128]{1,0:T(8,128)} %feat.1, f32[32,128]{1,0:T(8,128)} %bitcast.7, bf16[536,4096]{1,0:T(8,128)(2,1)} %bitcast.6, f32[1,24]{1,0:T(1,128)} %bias.1, bf16[64,768,128]{2,1,0:T(8,128)(2,1)} %bitcast.5, s32[1,64]{1,0:T(1,128)} %bitcast.8, f32[1,128]{1,0:T(1,128)} %bitcast.9, bf16[128,1024]{1,0:T(8,128)(2,1)} %outw.1), custom_call_target="tpu_custom_call" | custom-call | tf_op jit(solution)/shard_map/pallas_call | solution.py:268
  28.5 0.6 %copy.10 = f32[8,1024]{1,0:T(8,128)} copy(f32[8,1024]{1,0:T(8,128)S(1)} %shard_map.82) | data formatting | bytes 65536
where the time goes:
time: 29.3 us; the launch traced here: 29.2 us
  Pallas kernels  28.5 us (97%)
  local copies, waits for them, and re-layouts  0.62 us (2%)
    pallas_call x1, Pallas kernels, body(): pl.pallas_call(functools.partial(kernel, heads, levels, in_gain.shape[0],...  28.5 us
    unnamed x1, local copies, waits for them, and re-layouts  0.62 us

commit v1 on v0

--- a/solution.py
+++ b/solution.py
@@ -22,11 +22,15 @@
     )
 
 
+def arrived(shape_of, sem):
+    pltpu.make_async_copy(shape_of, shape_of, sem).wait()
+
+
 def kernel(
     heads, levels, width, dims,
-    feat, gain, inw, bias, states, pos, ogain, outw, out,
-    xbuf, wbuf, sbuf, owbuf, proj, abuf, bbuf, mbuf, osend, orecv, qfull, wnorm, qw, biasbuf, qsum,
-    x_sem, w_sem, s_sem, ow_sem, p1_send, p1_recv, a_send, a_recv, b_send, b_recv,
+    feat, gain_any, inw, bias_any, states, pos_any, ogain_any, outw, out,
+    gain, bias, pos, ogain, xbuf, wbuf, sbuf, owbuf, proj, abuf, bbuf, mbuf, osend, orecv, qfull, wnorm, qw, biasbuf, qsum,
+    small_sem, x_sem, w_sem, s_sem, ow_sem, p1_send, p1_recv, a_send, a_recv, b_send, b_recv,
     m_send, m_recv, o_send, o_recv, q_send, q_recv,
 ):
     key_dim, val_dim, level_total, level_here = dims
@@ -44,12 +48,6 @@
 
     x_copy = pltpu.make_async_copy(feat, xbuf.at[me_h], x_sem)
     x_copy.start()
-    w_copies = []
-    for h in range(heads):
-        start = pl.multiple_of((h * levels + me_l) * fw, fw)
-        part = inw.at[:, pl.ds(start, fw)] if flipped else inw.at[pl.ds(start, fw), :]
-        w_copies.append(pltpu.make_async_copy(part, wbuf.at[h], w_sem.at[h]))
-        w_copies[-1].start()
     last_group = (me_l * owned) // GROUP
     order = [lax.rem(last_group + 1 + t, groups) for t in range(groups)]
 
@@ -68,18 +66,25 @@
         pl.semaphore_signal(
             barrier, inc=1, device_id=(me_h, lax.rem(me_l + o, levels)),
             device_id_type=pl.DeviceIdType.MESH)
+    smalls = [
+        pltpu.make_async_copy(a, b, small_sem.at[i])
+        for i, (a, b) in enumerate(((gain_any, gain), (bias_any, bias), (pos_any, pos), (ogain_any, ogain)))]
+    for c in smalls:
+        c.start()
+    for h in range(heads):
+        start = pl.multiple_of((h * levels + me_l) * fw, fw)
+        part = inw.at[:, pl.ds(start, fw)] if flipped else inw.at[pl.ds(start, fw), :]
+        pltpu.make_async_copy(part, wbuf.at[h], w_sem).start()
     pl.semaphore_wait(barrier, heads + levels - 2)
 
     x_copy.wait()
-    pending = []
     buddy = me_h + 1 - 2 * lax.rem(me_h, 2)
     def feature_send(block, target, index):
-        c = send(xbuf.at[block], xbuf.at[block], p1_send.at[index], p1_recv.at[block], (target, me_l))
-        c.start()
-        pending.append(c)
+        c = send(xbuf.at[block], xbuf.at[block], p1_send, p1_recv.at[block], (target, me_l))
+        c.start()
 
     def feature_wait(block):
-        send(xbuf.at[block], xbuf.at[block], p1_send.at[0], p1_recv.at[block], (buddy, me_l)).wait_recv()
+        send(xbuf.at[block], xbuf.at[block], p1_send, p1_recv.at[block], (buddy, me_l)).wait_recv()
 
     chips, core = heads // 2, lax.rem(me_h, 2)
     mirror_chip = chips - 1 - me_h // 2
@@ -93,8 +98,9 @@
     for i, peer in enumerate(direct):
         feature_send(me_h, peer, i)
     feature_send(me_h, buddy, heads - 2)
-    for c in w_copies:
+    for c in smalls:
         c.wait()
+    arrived(wbuf, w_sem)
     acc = jnp.zeros((seqs, cols), jnp.float32)
     squares = jnp.zeros((seqs, 1), jnp.float32)
     arrivals = [me_h, buddy, mirror] + direct + [2 * mirror_chip + 1 - core]
@@ -126,16 +132,14 @@
     abuf[me_l, seqs:, :] = pack
     for o in range(1, levels):
         peer = lax.rem(me_l + o, levels)
-        c = send(abuf.at[me_l], abuf.at[me_l], a_send.at[o], a_recv.at[me_l], (me_h, peer))
-        c.start()
-        pending.append(c)
+        c = send(abuf.at[me_l], abuf.at[me_l], a_send, a_recv, (me_h, peer))
+        c.start()
     for o in range(1, levels):
         peer = lax.rem(me_l + o, levels)
         rows = pl.ds(pl.multiple_of(peer * owned, owned), owned)
         c = send(proj.at[rows, pl.ds(key_dim, tail0 - key_dim)], bbuf.at[me_l],
-                 b_send.at[o], b_recv.at[me_l], (me_h, peer))
-        c.start()
-        pending.append(c)
+                 b_send, b_recv, (me_h, peer))
+        c.start()
     mine = pl.ds(pl.multiple_of(me_l * owned, owned), owned)
     bbuf[me_l] = proj[mine, key_dim:tail0]
 
@@ -148,9 +152,7 @@
     bits = jnp.bitwise_and(jnp.right_shift(jnp.broadcast_to(pos_col, lane.shape), shift), 1)
     occupied = jnp.logical_and(lane < level_total, jnp.logical_or(lane == 0, bits == 1))
 
-    for o in range(1, levels):
-        src = lax.rem(me_l + levels - o, levels)
-        send(abuf.at[src], abuf.at[src], a_send.at[o], a_recv.at[src], (me_h, src)).wait_recv()
+    arrived(abuf.at[pl.ds(0, levels - 1)], a_recv)
     query = abuf[0, :seqs, :]
     pack = abuf[0, seqs:, :]
     for l in range(1, levels):
@@ -173,19 +175,16 @@
         qw[:, j * key_dim : (j + 1) * key_dim] = (query_low * local[:, j : j + 1]).astype(jnp.bfloat16)
 
     seq_in = lax.broadcasted_iota(jnp.int32, (GROUP, val_dim), 0)
-    def to_levels(rows, index):
+    def to_levels(rows):
         for o in range(1, levels):
             part = mbuf.at[me_l, rows, :]
-            c = send(part, part, m_send.at[o, index], m_recv.at[me_l, index],
+            c = send(part, part, m_send, m_recv,
                      (me_h, lax.rem(me_l + o, levels)))
             c.start()
-            pending.append(c)
 
     for t, g in enumerate(order):
         if t == groups - 1:
-            for o in range(1, levels):
-                src = lax.rem(me_l + levels - o, levels)
-                send(bbuf.at[src], bbuf.at[src], b_send.at[o], b_recv.at[src], (me_h, src)).wait_recv()
+            arrived(bbuf.at[pl.ds(0, levels - 1)], b_recv)
             rest = bbuf[0]
             for l in range(1, levels):
                 rest += bbuf[l]
@@ -194,7 +193,7 @@
             gate = rest[:, key_dim + val_dim :]
             own = jnp.sum(qfull[mine, :] * key, axis=1, keepdims=True) * key_dim ** (-0.5) * value
             mbuf[me_l, seqs:, :] = gate * jax.nn.sigmoid(gate)
-            to_levels(pl.ds(seqs, owned), groups)
+            to_levels(pl.ds(seqs, owned))
             qfull[...] = jnp.zeros(qfull.shape, jnp.float32)
             qfull[mine, :] = wnorm[mine, 0:1] * own
         state_copy(g).wait()
@@ -208,14 +207,9 @@
         if t == groups - 1:
             mixed += qfull[rows, :]
         mbuf[me_l, rows, :] = mixed
-        to_levels(rows, g)
+        to_levels(rows)
     ow_copy.wait()
-    for o in range(1, levels):
-        src = lax.rem(me_l + levels - o, levels)
-        for index in range(groups + 1):
-            rows = pl.ds(index * GROUP, GROUP if index < groups else owned)
-            part = mbuf.at[src, rows, :]
-            send(part, part, m_send.at[o, index], m_recv.at[src, index], (me_h, src)).wait_recv()
+    arrived(mbuf.at[pl.ds(0, levels - 1)], m_recv)
     gated = mbuf[0, :seqs, :]
     for l in range(1, levels):
         gated += mbuf[l, :seqs, :]
@@ -227,18 +221,15 @@
         osend[h] = product[h * out_rows : (h + 1) * out_rows]
     for o in range(1, heads):
         peer = lax.rem(me_h + o, heads)
-        c = send(osend.at[peer], orecv.at[me_h], o_send.at[o], o_recv.at[me_h], (peer, me_l))
-        c.start()
-        pending.append(c)
-        c = send(qsum.at[me_h], qsum.at[me_h], q_send.at[o], q_recv.at[me_h], (peer, me_l))
-        c.start()
-        pending.append(c)
+        c = send(osend.at[peer], orecv.at[me_h], o_send, o_recv, (peer, me_l))
+        c.start()
+        c = send(qsum.at[me_h], qsum.at[me_h], q_send, q_recv, (peer, me_l))
+        c.start()
     total = osend[me_h]
+    arrived(orecv.at[pl.ds(0, heads - 1)], o_recv)
+    arrived(qsum.at[pl.ds(0, heads - 1)], q_recv)
     for o in range(1, heads):
-        src = lax.rem(me_h + heads - o, heads)
-        send(osend.at[src], orecv.at[src], o_send.at[o], o_recv.at[src], (src, me_l)).wait_recv()
-        send(qsum.at[src], qsum.at[src], q_send.at[o], q_recv.at[src], (src, me_l)).wait_recv()
-        total += orecv[src]
+        total += orecv[lax.rem(me_h + heads - o, heads)]
     all_sq = qsum[0]
     for h in range(1, heads):
         all_sq += qsum[h]
@@ -246,8 +237,12 @@
     pick = lax.broadcasted_iota(jnp.int32, (out_rows, seqs), 1) == here
     mean = jnp.sum(jnp.where(pick, jnp.broadcast_to(all_sq, pick.shape), 0.0), axis=1, keepdims=True) / (heads * val_dim)
     out[...] = total * lax.rsqrt(mean + 1e-05)
-    for c in pending:
-        c.wait_send()
+    arrived(xbuf.at[pl.ds(0, heads - 1)], p1_send)
+    arrived(abuf.at[pl.ds(0, levels - 1)], a_send)
+    arrived(bbuf.at[pl.ds(0, levels - 1)], b_send)
+    arrived(mbuf.at[pl.ds(0, levels - 1)], m_send)
+    arrived(orecv.at[pl.ds(0, heads - 1)], o_send)
+    arrived(qsum.at[pl.ds(0, heads - 1)], q_send)
 
 
 def body(features, in_gain, in_weight, level_bias, states, positions, out_gain, out_weight):
@@ -268,9 +263,13 @@
     return pl.pallas_call(
         functools.partial(kernel, heads, levels, in_gain.shape[0], (key_dim, val_dim, level_total, level_here)),
         out_shape=pltpu.VMEM((out_rows, out_cols), f32),
-        in_specs=[anyspace, vmem, anyspace, vmem, anyspace, vmem, vmem, anyspace],
+        in_specs=[anyspace] * 8,
         out_specs=vmem,
         scratch_shapes=[
+            pltpu.VMEM((heads * levels, fw), f32),
+            pltpu.VMEM(level_bias.shape, f32),
+            pltpu.VMEM((1, seqs), jnp.int32),
+            pltpu.VMEM((1, val_dim), f32),
             pltpu.VMEM((heads, seqs, fw), f32),
             pltpu.VMEM((heads, cols, fw) if flipped else (heads, fw, cols), bf16),
             pltpu.VMEM((seqs, level_here * key_dim, val_dim), bf16),
@@ -286,11 +285,9 @@
             pltpu.VMEM((seqs, level_here * key_dim), bf16),
             pltpu.VMEM((1, LANES), f32),
             pltpu.VMEM((heads, 1, seqs), f32),
-            dma(()), dma((heads,)), dma((seqs // GROUP,)), dma(()),
-            dma((heads,)), dma((heads,)),
-            dma((levels,)), dma((levels,)), dma((levels,)), dma((levels,)),
-            dma((levels, seqs // GROUP + 1)), dma((levels, seqs // GROUP + 1)),
-            dma((heads,)), dma((heads,)), dma((heads,)), dma((heads,)),
+            dma((4,)), dma(()), dma(()), dma((seqs // GROUP,)), dma(()),
+            dma(()), dma((heads,)),
+            *[dma(())] * 10,
         ],
         compiler_params=pltpu.CompilerParams(collective_id=0, has_side_effects=True),
     )(

time: 29.3 us -> 27.7 us (0.945)
  Pallas kernels: 28.5 us -> 26.9 us
    pallas_call x1, Pallas kernels: 28.5 us -> 26.9 us  [body(): pl.pallas_call(functools.partial(kernel, heads, levels, in_gain.shape[0],...]
where the time goes in v1:
time: 27.7 us; the launch traced here: 27.5 us
  Pallas kernels  26.9 us (97%)
  local copies, waits for them, and re-layouts  0.62 us (2%)
    pallas_call x1, Pallas kernels, body(): pl.pallas_call(functools.partial(kernel, heads, levels, in_gain.shape[0],...  26.9 us
    unnamed x1, local copies, waits for them, and re-layouts  0.62 us

profile of v1, /device:TPU:0, one launch (start us, length us, event | category | flops | bytes accessed | tf_op | source)
XLA Modules:
  0.0 27.5 jit_solution(7875205381184632299)
XLA Ops:
  0.0 26.9 %shard_map.82 = f32[8,1024]{1,0:T(8,128)S(1)} custom-call(f32[64,128]{1,0:T(8,128)} %feat.1, f32[32,128]{1,0:T(8,128)} %bitcast.7, bf16[536,4096]{1,0:T(8,128)(2,1)} %bitcast.6, f32[1,24]{1,0:T(1,128)} %bias_any.1, bf16[64,768,128]{2,1,0:T(8,128)(2,1)} %bitcast.5, s32[1,64]{1,0:T(1,128)} %bitcast.8, f32[1,128]{1,0:T(1,128)} %bitcast.9, bf16[128,1024]{1,0:T(8,128)(2,1)} %outw.1), custom_call_target="tpu_custom_call" | custom-call | tf_op jit(solution)/shard_map/pallas_call | solution.py:263
  26.9 0.6 %copy.10 = f32[8,1024]{1,0:T(8,128)} copy(f32[8,1024]{1,0:T(8,128)S(1)} %shard_map.82) | data formatting | bytes 65536

commit v2 on v1

v2 whole, which is shorter than its diff:
```python
import functools

import jax
import jax.numpy as jnp
from jax import lax
from jax.experimental import pallas as pl
from jax.experimental.pallas import tpu as pltpu
from jax.sharding import PartitionSpec as P

LANES = 128
GROUP = 16


def send(src, dst, send_sem, recv_sem, target):
    c = pltpu.make_async_remote_copy(
        src_ref=src,
        dst_ref=dst,
        send_sem=send_sem,
        recv_sem=recv_sem,
        device_id=target,
        device_id_type=pl.DeviceIdType.MESH,
    )
    c.start()


def arrived(like, sem):
    pltpu.make_async_copy(like, like, sem).wait()


def flip_bits(value, mask, count):
    result, bit = 0, 1
    while bit < count:
        own = lax.rem(value // bit, 2)
        result = result + bit * (1 - own if mask & bit else own)
        bit *= 2
    return result


def kernel(
    heads, levels, width, dims,
    feat, gain_any, inw, bias_any, states, pos_any, ogain_any, outw, out,
    gain, bias, pos, ogain, xbuf, wbuf, sbuf, owbuf, tailbuf, tbuf, qbuf, kx, xk, keys, values, gates,
    wexp, scales, mbuf, osend, orecv, biasbuf,
    small_sem, x_sem, w_sem, s_sem, ow_sem, f_send, f_recv, kx_send, kx_recv, k2_send, k2_recv,
    t_send, t_recv, q_send, q_recv, g_send, g_recv, m_send, m_recv, o_send, o_recv,
):
    key_dim, val_dim, level_total, level_here = dims
    seqs, fw = feat.shape
    flipped = fw % LANES == 0
    owned = seqs // levels
    out_rows = seqs // heads
    out_cols = outw.shape[1]
    me_h, me_l = lax.axis_index("head"), lax.axis_index("level")
    slot = 1 << level_total.bit_length()
    slots = LANES // slot
    packed = seqs // slots
    groups = seqs // GROUP
    per = heads // groups
    block, me_j = me_h // per, lax.rem(me_h, per)
    order = [flip_bits(block, groups - 1 - t, groups) for t in range(groups)]
    mine = pl.ds(pl.multiple_of(me_l * owned, owned), owned)
    peers = [lax.rem(me_l + o, levels) for o in range(1, levels)]
    tail0 = 2 * key_dim + 2 * val_dim
    f32, bf16 = jnp.float32, jnp.bfloat16

    def group_rows(t):
        return pl.ds(pl.multiple_of(order[t] * GROUP, GROUP), GROUP)

    x_copy = pltpu.make_async_copy(feat, xbuf.at[me_h], x_sem)
    x_copy.start()

    barrier = pltpu.get_barrier_semaphore()
    for o in range(1, heads):
        pl.semaphore_signal(
            barrier, inc=1, device_id=(lax.rem(me_h + o, heads), me_l),
            device_id_type=pl.DeviceIdType.MESH)
    for peer in peers:
        pl.semaphore_signal(
            barrier, inc=1, device_id=(me_h, peer), device_id_type=pl.DeviceIdType.MESH)
    smalls = [
        pltpu.make_async_copy(a, b, small_sem.at[i])
        for i, (a, b) in enumerate(((gain_any, gain), (bias_any, bias), (pos_any, pos), (ogain_any, ogain)))]
    for c in smalls:
        c.start()
    w_copy = pltpu.make_async_copy(inw, wbuf, w_sem)
    w_copy.start()
    pl.semaphore_wait(barrier, heads + levels - 2)

    x_copy.wait()
    buddy = me_h + 1 - 2 * lax.rem(me_h, 2)

    def feature_send(source, target):
        send(xbuf.at[source], xbuf.at[source], f_send, f_recv.at[source], (target, me_l))

    def feature_wait(source):
        arrived(xbuf.at[source], f_recv.at[source])

    chips, core = heads // 2, lax.rem(me_h, 2)
    mirror_chip = chips - 1 - me_h // 2
    skip = lax.rem(me_h // 2 - mirror_chip + chips, chips)
    mirror = 2 * mirror_chip + core
    direct = []
    for j in range(1, chips - 1):
        near = 2 * lax.rem(mirror_chip + j + (j + chips - skip) // chips, chips)
        direct += [near + core, near + 1 - core]
    feature_send(me_h, mirror)
    for peer in direct:
        feature_send(me_h, peer)
    feature_send(me_h, buddy)
    for o, peer in enumerate(peers, 1):
        theirs = pl.ds(pl.multiple_of(peer * owned, owned), owned)
        send(xbuf.at[me_h, theirs], kx.at[levels - 1 - o, me_h], kx_send, kx_recv, (me_h, peer))
    for c in smalls:
        c.wait()
    w_copy.wait()

    def weight(first, last, start, size):
        if flipped:
            return wbuf[first:last, pl.ds(start, size)]
        return wbuf[pl.ds(start, size), first:last]

    def project(x, w):
        return lax.dot_general(x, w, (((1,), (1 if flipped else 0,)), ((), ())), preferred_element_type=f32)

    query = jnp.zeros((seqs, key_dim), f32)
    tail = jnp.zeros((seqs, level_total), f32)
    squares = jnp.zeros((seqs, fw), f32)
    arrivals = [me_h, buddy, mirror] + direct + [2 * mirror_chip + 1 - core]
    for i, src in enumerate(arrivals):
        if i:
            feature_wait(src)
        if i == 2:
            feature_send(mirror, buddy)
        x = xbuf[src]
        index = src * levels + me_l
        start = pl.multiple_of(index * fw, fw)
        scaled = (x * gain[pl.ds(index, 1), :]).astype(bf16)
        query += project(scaled, weight(0, key_dim, start, fw))
        tail += project(scaled, weight(tail0, tail0 + level_total, start, fw))
        squares += x * x
    squares = jnp.sum(squares, axis=1, keepdims=True)

    tailbuf[:, :level_total] = tail
    lane = lax.broadcasted_iota(jnp.int32, (seqs, LANES), 1)
    tail = jnp.where(lane < level_total, tailbuf[...], 0.0)
    tail = jnp.where(lane == level_total, squares, tail)
    pack = tail[:packed]
    for c in range(1, slots):
        pack += pltpu.roll(tail[c * packed : (c + 1) * packed], slot * c, 1)
    tbuf[me_l] = pack
    qbuf[me_l] = query
    for peer in peers:
        send(tbuf.at[me_l], tbuf.at[me_l], t_send, t_recv, (me_h, peer))
    for t in range(groups):
        part = qbuf.at[me_l, group_rows(t)]
        for peer in peers:
            send(part, part, q_send, q_recv.at[t], (me_h, peer))

    arrived(kx.at[:, 0], kx_recv)
    for o in range(1, heads):
        part = kx.at[:, me_h]
        send(part, part, k2_send, k2_recv, (lax.rem(me_h + o, heads), me_l))

    def state_copy(t):
        rows = group_rows(t)
        return pltpu.make_async_copy(states.at[rows], sbuf.at[rows], s_sem.at[t])

    for t in range(groups):
        state_copy(t).start()
    ow_copy = pltpu.make_async_copy(outw, owbuf, ow_sem)
    ow_copy.start()

    keys[...] = jnp.zeros(keys.shape, f32)
    values[...] = jnp.zeros(values.shape, f32)
    biasbuf[:, :level_total] = bias[...]
    row = lax.broadcasted_iota(jnp.int32, (seqs, seqs), 0)
    col = lax.broadcasted_iota(jnp.int32, (seqs, seqs), 1)
    pos_f = jnp.broadcast_to(pos[...], (seqs, seqs)).astype(f32)
    pos_col = jnp.sum(jnp.where(row == col, pos_f, 0.0), axis=1, keepdims=True).astype(jnp.int32)
    shift = jnp.clip(lane - 1, 0, 31)
    bits = jnp.bitwise_and(jnp.right_shift(jnp.broadcast_to(pos_col, lane.shape), shift), 1)
    occupied = jnp.logical_and(lane < level_total, jnp.logical_or(lane == 0, bits == 1))

    arrived(tbuf.at[pl.ds(0, levels - 1)], t_recv)
    pack = tbuf[0]
    for l in range(1, levels):
        pack += tbuf[l]
    parts = [pack] + [pltpu.roll(pack, LANES - slot * c, 1) for c in range(1, slots)]
    tail = jnp.concatenate(parts, axis=0)
    row_scale = lax.rsqrt(tail[:, level_total : level_total + 1] / width + 1e-06)
    logits = tail * row_scale + biasbuf[...]
    peak = jnp.max(jnp.where(occupied, logits, -1e30), axis=1, keepdims=True)
    weights = jnp.where(occupied, jnp.exp(logits - peak), 0.0)
    weights = weights / jnp.sum(weights, axis=1, keepdims=True)
    local = pltpu.roll(weights, lax.rem(LANES - me_l * level_here, LANES), 1)
    for j in range(level_here):
        wexp[:, j * key_dim : (j + 1) * key_dim] = jnp.broadcast_to(local[:, j : j + 1], (seqs, key_dim))
    scales[:, :LANES] = jnp.broadcast_to(row_scale, weights.shape)
    scales[:, LANES:] = jnp.broadcast_to(weights[:, :1], weights.shape)

    arrived(kx.at[:, pl.ds(0, heads - 1)], k2_recv)
    if flipped:
        squares = jnp.zeros((owned, fw), f32)
        for h in range(heads):
            for o in range(levels):
                x = kx[o - 1, h] if o else xbuf[h, mine, :]
                index = h * levels + lax.rem(me_l + o, levels)
                xk[:, pl.ds(pl.multiple_of(index * fw, fw), fw)] = (x * gain[pl.ds(index, 1), :]).astype(bf16)
                squares += x * x
        rest = project(xk[...], wbuf[key_dim:tail0, :])
    else:
        def part(h, carry):
            rest, squares = carry
            for o in range(levels):
                x = kx[o - 1, h] if o else xbuf[h, mine, :]
                index = h * levels + lax.rem(me_l + o, levels)
                start = pl.multiple_of(index * fw, fw)
                scaled = (x * gain[pl.ds(index, 1), :]).astype(bf16)
                rest = rest + project(scaled, weight(key_dim, tail0, start, fw))
                squares = squares + x * x
            return rest, squares

        rest, squares = lax.fori_loop(
            0, heads, part, (jnp.zeros((owned, tail0 - key_dim), f32), jnp.zeros((owned, fw), f32)))
    rest = rest * lax.rsqrt(jnp.sum(squares, axis=1, keepdims=True) / width + 1e-06)
    gate = rest[:, key_dim + val_dim :]
    keys[mine, :] = rest[:, :key_dim]
    values[mine, :] = rest[:, key_dim : key_dim + val_dim] * key_dim ** (-0.5)
    gates[mine, :] = gate * jax.nn.sigmoid(gate)
    for peer in peers:
        send(gates.at[mine], gates.at[mine], g_send, g_recv, (me_h, peer))

    seq_in = lax.broadcasted_iota(jnp.int32, (GROUP, val_dim), 0)
    for t in range(groups):
        rows = group_rows(t)
        arrived(qbuf.at[pl.ds(0, levels - 1), pl.ds(0, GROUP)], q_recv.at[t])
        query = qbuf[0, rows, :]
        for l in range(1, levels):
            query += qbuf[l, rows, :]
        query = query * scales[rows, :LANES]
        low = query.astype(bf16).astype(f32)
        left = jnp.concatenate(
            [(low * wexp[rows, j * key_dim : (j + 1) * key_dim]).astype(bf16) for j in range(level_here)], axis=1)
        own = jnp.sum(query * keys[rows, :], axis=1, keepdims=True) * values[rows, :]
        mixed = scales[rows, LANES:] * own
        state_copy(t).wait()
        base = pl.multiple_of(order[t] * GROUP, GROUP)
        reads = jnp.zeros((GROUP, val_dim), f32)
        for i in range(GROUP):
            got = jnp.dot(left, sbuf[base + i], preferred_element_type=f32)
            reads = jnp.where(seq_in == i, got, reads)
        mbuf[me_l, rows, :] = mixed + reads
        part = mbuf.at[me_l, rows]
        for peer in peers:
            send(part, part, m_send, m_recv.at[t], (me_h, peer))

    ow_copy.wait()
    arrived(gates.at[pl.ds(0, seqs - owned)], g_recv)
    for t in range(groups):
        rows = group_rows(t)
        arrived(mbuf.at[pl.ds(0, levels - 1), pl.ds(0, GROUP)], m_recv.at[t])
        gated = mbuf[0, rows, :]
        for l in range(1, levels):
            gated += mbuf[l, rows, :]
        gated = gated * gates[rows, :]
        total_sq = jnp.broadcast_to(jnp.sum(gated * gated, axis=1, keepdims=True), (GROUP, LANES))
        product = jnp.dot((gated * ogain[...]).astype(bf16), owbuf[...], preferred_element_type=f32)
        for j in range(per):
            osend[t, j, :, :out_cols] = product[j * out_rows : (j + 1) * out_rows]
            osend[t, j, :, out_cols:] = total_sq[j * out_rows : (j + 1) * out_rows]
        if t < groups - 1:
            for j in range(per):
                send(osend.at[t, j], orecv.at[me_h], o_send, o_recv, (order[t] * per + j, me_l))
        else:
            for o in range(1, per):
                j = lax.rem(me_j + o, per)
                send(osend.at[t, j], orecv.at[me_h], o_send, o_recv, (block * per + j, me_l))
    total = osend[groups - 1, me_j]
    arrived(orecv.at[pl.ds(0, heads - 1)], o_recv)
    for o in range(1, heads):
        total += orecv[lax.rem(me_h + heads - o, heads)]
    mean = total[:, out_cols : out_cols + 1] / (heads * val_dim)
    out[...] = total[:, :out_cols] * lax.rsqrt(mean + 1e-05)
    arrived(xbuf.at[pl.ds(0, heads - 1)], f_send)
    arrived(kx.at[:, 0], kx_send)
    arrived(kx.at[:, pl.ds(0, heads - 1)], k2_send)
    arrived(tbuf.at[pl.ds(0, levels - 1)], t_send)
    arrived(qbuf.at[pl.ds(0, levels - 1)], q_send)
    arrived(gates.at[pl.ds(0, seqs - owned)], g_send)
    arrived(mbuf.at[pl.ds(0, levels - 1)], m_send)
    arrived(orecv.at[pl.ds(0, heads - 1)], o_send)


def body(features, in_gain, in_weight, level_bias, states, positions, out_gain, out_weight):
    heads, levels = lax.axis_size("head"), lax.axis_size("level")
    seqs, fw = features.shape
    width, cols = in_weight.shape
    _, head_here, level_here, key_dim, val_dim = states.shape
    level_total = level_bias.shape[1]
    assert head_here == 1 and key_dim == LANES and val_dim == LANES
    out_cols = out_weight.shape[1]
    flipped = fw % LANES == 0
    slots = LANES // (1 << level_total.bit_length())
    owned, out_rows, groups = seqs // levels, seqs // heads, seqs // GROUP
    f32, bf16 = jnp.float32, jnp.bfloat16
    vmem, anyspace = pl.BlockSpec(memory_space=pltpu.VMEM), pl.BlockSpec(memory_space=pl.ANY)
    dma = pltpu.SemaphoreType.DMA
    return pl.pallas_call(
        functools.partial(kernel, heads, levels, in_gain.shape[0], (key_dim, val_dim, level_total, level_here)),
        out_shape=pltpu.VMEM((out_rows, out_cols), f32),
        in_specs=[anyspace] * 8,
        out_specs=vmem,
        scratch_shapes=[
            pltpu.VMEM((heads * levels, fw), f32),
            pltpu.VMEM(level_bias.shape, f32),
            pltpu.VMEM((1, seqs), jnp.int32),
            pltpu.VMEM((1, val_dim), f32),
            pltpu.VMEM((heads, seqs, fw), f32),
            pltpu.VMEM((cols, width) if flipped else (width, cols), bf16),
            pltpu.VMEM((seqs, level_here * key_dim, val_dim), bf16),
            pltpu.VMEM(out_weight.shape, bf16),
            pltpu.VMEM((seqs, LANES), f32),
            pltpu.VMEM((levels, seqs // slots, LANES), f32),
            pltpu.VMEM((levels, seqs, key_dim), f32),
            pltpu.VMEM((levels - 1, heads, owned, fw), f32),
            pltpu.VMEM((owned, width), bf16),
            pltpu.VMEM((seqs, key_dim), f32),
            pltpu.VMEM((seqs, val_dim), f32),
            pltpu.VMEM((seqs, val_dim), f32),
            pltpu.VMEM((seqs, level_here * key_dim), f32),
            pltpu.VMEM((seqs, 2 * LANES), f32),
            pltpu.VMEM((levels, seqs, val_dim), f32),
            pltpu.VMEM((groups, heads // groups, out_rows, out_cols + LANES), f32),
            pltpu.VMEM((heads, out_rows, out_cols + LANES), f32),
            pltpu.VMEM((1, LANES), f32),
            dma((4,)), dma(()), dma(()), dma((groups,)), dma(()),
            dma(()), dma((heads,)), *[dma(())] * 4,
            dma(()), dma(()), dma(()), dma((groups,)), dma(()), dma(()), dma(()), dma((groups,)), dma(()), dma(()),
        ],
        compiler_params=pltpu.CompilerParams(collective_id=0, has_side_effects=True),
    )(
        features,
        in_gain.reshape(heads * levels, fw),
        in_weight.T if flipped else in_weight,
        level_bias,
        states.reshape(seqs, level_here * key_dim, val_dim),
        positions.reshape(1, seqs),
        out_gain.reshape(1, val_dim),
        out_weight,
    )


def solution(mesh):
    in_specs = (
        P(None, ("head", "level")),
        P(),
        P(None, "head"),
        P("head", None),
        P(None, "head", "level", None, None),
        P(),
        P("head"),
        P("head", "level"),
    )
    out_specs = P("head", "level")
    return jax.shard_map(body, mesh=mesh, in_specs=in_specs, out_specs=out_specs, check_vma=False)
```

time: 27.7 us -> 25.8 us (0.931)
  Pallas kernels: 26.9 us -> 25.1 us
    pallas_call x1, Pallas kernels: 26.9 us -> 25.1 us  [body(): pl.pallas_call(functools.partial(kernel, heads, levels, in_gain.shape[0],...]
where the time goes in v2:
time: 25.8 us; the launch traced here: 25.7 us
  Pallas kernels  25.1 us (97%)
  local copies, waits for them, and re-layouts  0.62 us (2%)
    pallas_call x1, Pallas kernels, body(): pl.pallas_call(functools.partial(kernel, heads, levels, in_gain.shape[0],...  25.1 us
    unnamed x1, local copies, waits for them, and re-layouts  0.62 us

profile of v2, /device:TPU:0, one launch (start us, length us, event | category | flops | bytes accessed | tf_op | source)
XLA Modules:
  0.0 25.7 jit_solution(1741381346484051565)
XLA Ops:
  0.0 25.1 %shard_map.82 = f32[8,1024]{1,0:T(8,128)S(1)} custom-call(f32[64,128]{1,0:T(8,128)} %feat.1, f32[32,128]{1,0:T(8,128)} %bitcast.7, bf16[536,4096]{1,0:T(8,128)(2,1)} %bitcast.6, f32[1,24]{1,0:T(1,128)} %bias_any.1, bf16[64,768,128]{2,1,0:T(8,128)(2,1)} %bitcast.5, s32[1,64]{1,0:T(1,128)} %bitcast.8, f32[1,128]{1,0:T(1,128)} %bitcast.9, bf16[128,1024]{1,0:T(8,128)(2,1)} %outw.1), custom_call_target="tpu_custom_call" | custom-call | tf_op jit(solution)/shard_map/pallas_call | solution.py:308
  25.1 0.6 %copy.10 = f32[8,1024]{1,0:T(8,128)} copy(f32[8,1024]{1,0:T(8,128)S(1)} %shard_map.82) | data formatting | bytes 65536

commit v3 on v2

v3 whole, which is shorter than its diff:
```python
import functools

import jax
import jax.numpy as jnp
from jax import lax
from jax.experimental import pallas as pl
from jax.experimental.pallas import tpu as pltpu
from jax.sharding import PartitionSpec as P

LANES = 128
GROUP = 16
POSITION_BITS = 18


def send(src, dst, send_sem, recv_sem, target):
    c = pltpu.make_async_remote_copy(
        src_ref=src,
        dst_ref=dst,
        send_sem=send_sem,
        recv_sem=recv_sem,
        device_id=target,
        device_id_type=pl.DeviceIdType.MESH,
    )
    c.start()


def arrived(like, sem):
    pltpu.make_async_copy(like, like, sem).wait()


def exclusive_or(a, b, count):
    result, bit = 0, 1
    while bit < count:
        result = result + bit * lax.rem(a // bit + b // bit, 2)
        bit *= 2
    return result


def kernel(
    heads, levels, width, dims,
    feat, gain_any, inw, bias_any, states, pos_any, ogain_any, outw, out,
    gain, bias, pos, ogain, xbuf, wbuf, sbuf, owbuf, tailbuf, tbuf, qbuf, qtmp, kx, gates, restbuf, sqbuf, ownbuf,
    wexp, scales, mbuf, osend, orecv, biasbuf,
    z_sem, small_sem, x_sem, w_sem, s_sem, ow_sem, sent, f_recv, kx_recv, k2_recv,
    t_recv, q_recv, g_recv, m_recv, o_recv,
):
    key_dim, val_dim, level_total, level_here = dims
    seqs, fw = feat.shape
    flipped = fw % LANES == 0
    owned = seqs // levels
    out_rows = seqs // heads
    out_cols = outw.shape[1]
    me_h, me_l = lax.axis_index("head"), lax.axis_index("level")
    slot = 1 << level_total.bit_length()
    slots = LANES // slot
    packed = seqs // slots
    groups = seqs // GROUP
    per = heads // groups
    block, me_j = me_h // per, lax.rem(me_h, per)
    order = [exclusive_or(block, groups - 1 - t, groups) for t in range(groups)]
    my_block = me_l * owned // GROUP
    my_t = groups - 1 - exclusive_or(block, my_block, groups)
    own_rows = pl.ds(pl.multiple_of(my_t * GROUP + lax.rem(me_l * owned, GROUP), owned), owned)
    mine = pl.ds(pl.multiple_of(me_l * owned, owned), owned)
    peers = [l + jnp.where(me_l <= l, 1, 0) for l in range(levels - 1)]

    def by_level(choice):
        value = jnp.int32(choice(0))
        for l in range(1, levels):
            value = jnp.where(me_l == l, choice(l), value)
        return value

    tail0 = 2 * key_dim + 2 * val_dim
    f32, bf16 = jnp.float32, jnp.bfloat16

    def group_rows(t):
        return pl.ds(pl.multiple_of(order[t] * GROUP, GROUP), GROUP)

    def rows_of_group(ref, t, first=0, last=LANES):
        return ref[group_rows(t), first:last]

    x_copy = pltpu.make_async_copy(feat, xbuf.at[me_h], x_sem)
    x_copy.start()

    def tell(sem, h, l):
        pl.semaphore_signal(sem, inc=1, device_id=(h, l), device_id_type=pl.DeviceIdType.MESH)

    core = lax.rem(me_h, 2)
    buddy = me_h + 1 - 2 * core
    barrier = pltpu.get_barrier_semaphore()
    pl.loop(me_l + 1, levels)(lambda l: tell(barrier, me_h, l))
    for o in range(1, heads):
        tell(barrier, lax.rem(me_h + o, heads), me_l)
    smalls = [
        pltpu.make_async_copy(a, b, small_sem.at[i])
        for i, (a, b) in enumerate(((gain_any, gain), (bias_any, bias), (pos_any, pos), (ogain_any, ogain)))]
    for c in smalls:
        c.start()
    if flipped:
        for l in range(levels):
            for h in range(heads):
                pltpu.make_async_copy(
                    inw.at[:, pl.ds((h * levels + l) * fw, fw)], wbuf.at[:, pl.ds((l * heads + h) * fw, fw)], w_sem).start()
    else:
        pltpu.make_async_copy(inw, wbuf, w_sem).start()
    pl.semaphore_wait(barrier, heads - 1 + me_l)
    pl.loop(0, me_l)(lambda l: tell(z_sem, me_h, l))

    x_copy.wait()

    def feature_send(source, target):
        send(xbuf.at[source], xbuf.at[source], sent, f_recv.at[source], (target, me_l))

    def feature_wait(source):
        arrived(xbuf.at[source], f_recv.at[source])

    chips = heads // 2
    mirror_chip = chips - 1 - me_h // 2
    skip = lax.rem(me_h // 2 - mirror_chip + chips, chips)
    mirror = 2 * mirror_chip + core
    direct = []
    for j in range(1, chips - 1):
        near = 2 * lax.rem(mirror_chip + j + (j + chips - skip) // chips, chips)
        direct += [near + core, near + 1 - core]
    feature_send(me_h, mirror)
    for peer in direct:
        feature_send(me_h, peer)
    feature_send(me_h, buddy)

    def rows_send(l):
        theirs = pl.ds(pl.multiple_of(l * owned, owned), owned)
        send(xbuf.at[me_h, theirs], kx.at[me_l, me_h], sent, kx_recv.at[me_l], (me_h, l))

    pl.loop(0, me_l)(rows_send)
    for c in smalls:
        c.wait()
    arrived(wbuf, w_sem)

    def weight(first, last, h, l):
        if flipped:
            return wbuf[first:last, pl.ds(pl.multiple_of((l * heads + h) * fw, fw), fw)]
        return wbuf[pl.ds(pl.multiple_of((h * levels + l) * fw, fw), fw), first:last]

    def project(x, w):
        return lax.dot_general(x, w, (((1,), (1 if flipped else 0,)), ((), ())), preferred_element_type=f32)

    query = jnp.zeros((seqs, key_dim), f32)
    tail = jnp.zeros((seqs, level_total), f32)
    squares = jnp.zeros((seqs, fw), f32)
    arrivals = [me_h, buddy, mirror] + direct + [2 * mirror_chip + 1 - core]
    for i, src in enumerate(arrivals):
        if i == len(arrivals) - 2:
            @pl.when(me_l < levels - 1)
            def _():
                pl.semaphore_wait(z_sem, levels - 1 - me_l)

            pl.loop(me_l + 1, levels)(rows_send)
        if i:
            feature_wait(src)
        if i == 2:
            feature_send(mirror, buddy)
        x = xbuf[src]
        index = src * levels + me_l
        scaled = (x * gain[pl.ds(index, 1), :]).astype(bf16)
        query += project(scaled, weight(0, key_dim, src, me_l))
        tail += project(scaled, weight(tail0, tail0 + level_total, src, me_l))
        squares += x * x
    squares = jnp.sum(squares, axis=1, keepdims=True)

    tailbuf[:, :level_total] = tail
    lane = lax.broadcasted_iota(jnp.int32, (seqs, LANES), 1)
    tail = jnp.where(lane < level_total, tailbuf[...], 0.0)
    tail = jnp.where(lane == level_total, squares, tail)
    pack = tail[:packed]
    for c in range(1, slots):
        pack += pltpu.roll(tail[c * packed : (c + 1) * packed], slot * c, 1)
    tbuf[me_l] = pack
    qtmp[...] = query
    for t in range(groups):
        qbuf[me_l, t * GROUP : (t + 1) * GROUP] = rows_of_group(qtmp, t)
    for peer in peers:
        send(tbuf.at[me_l], tbuf.at[me_l], sent, t_recv, (me_h, peer))
    for t in range(groups):
        part = qbuf.at[me_l, pl.ds(t * GROUP, GROUP)]
        for peer in peers:
            send(part, part, sent, q_recv.at[t], (me_h, peer))

    possible = min(level_total, POSITION_BITS + 1)
    counts = sorted({min(max(possible - l * level_here, 0), level_here) for l in range(levels)})
    count = jnp.clip(possible - me_l * level_here, 0, level_here)

    def state_start(t, n):
        part = (group_rows(t), pl.ds(0, n * key_dim))
        pltpu.make_async_copy(states.at[part], sbuf.at[part], s_sem).start()

    for n in counts:
        @pl.when(jnp.logical_and(count == n, n > 0))
        def _():
            for t in range(groups):
                state_start(t, n)

    ow_copy = pltpu.make_async_copy(outw, owbuf, ow_sem)
    ow_copy.start()

    biasbuf[:, :level_total] = bias[...]
    row = lax.broadcasted_iota(jnp.int32, (seqs, seqs), 0)
    col = lax.broadcasted_iota(jnp.int32, (seqs, seqs), 1)
    pos_f = jnp.broadcast_to(pos[...], (seqs, seqs)).astype(f32)
    pos_col = jnp.sum(jnp.where(row == col, pos_f, 0.0), axis=1, keepdims=True).astype(jnp.int32)
    shift = jnp.clip(lane - 1, 0, 31)
    bits = jnp.bitwise_and(jnp.right_shift(jnp.broadcast_to(pos_col, lane.shape), shift), 1)
    occupied = jnp.logical_and(lane < level_total, jnp.logical_or(lane == 0, bits == 1))

    def piece(l, rows_of):
        total = jnp.zeros((owned, fw), f32)
        if flipped:
            scaled = []
            for h in range(heads):
                x = rows_of(h)
                scaled.append((x * gain[pl.ds(h * levels + l, 1), :]).astype(bf16))
                total += x * x
            at = pl.ds(pl.multiple_of(l * heads * fw, heads * fw), heads * fw)
            return project(jnp.concatenate(scaled, axis=1), wbuf[key_dim:tail0, at]), total

        def step(h, carry):
            rest, total = carry
            x = rows_of(h)
            scaled = (x * gain[pl.ds(h * levels + l, 1), :]).astype(bf16)
            return rest + project(scaled, weight(key_dim, tail0, h, l)), total + x * x

        return lax.fori_loop(0, heads, step, (jnp.zeros((owned, tail0 - key_dim), f32), total))

    restbuf[...], sqbuf[...] = piece(me_l, lambda h: xbuf[h, mine, :])
    for s in range(levels - 1):
        l = by_level(lambda me: sorted((p for p in range(levels) if p != me), key=lambda p: (abs(p - me), p))[s])
        arrived(kx.at[0, 0], kx_recv.at[l])
        part = kx.at[l, me_h]
        for target in [mirror, 2 * mirror_chip + 1 - core] + direct + [buddy]:
            send(part, part, sent, k2_recv, (target, me_l))

    arrived(tbuf.at[pl.ds(0, levels - 1)], t_recv)
    pack = tbuf[0]
    for l in range(1, levels):
        pack += tbuf[l]
    parts = [pack] + [pltpu.roll(pack, LANES - slot * c, 1) for c in range(1, slots)]
    tail = jnp.concatenate(parts, axis=0)
    row_scale = lax.rsqrt(tail[:, level_total : level_total + 1] / width + 1e-06)
    logits = tail * row_scale + biasbuf[...]
    peak = jnp.max(jnp.where(occupied, logits, -1e30), axis=1, keepdims=True)
    weights = jnp.where(occupied, jnp.exp(logits - peak), 0.0)
    weights = weights / jnp.sum(weights, axis=1, keepdims=True)
    local = pltpu.roll(weights, lax.rem(LANES - me_l * level_here, LANES), 1)
    for j in range(level_here):
        wexp[:, j * key_dim : (j + 1) * key_dim] = jnp.broadcast_to(local[:, j : j + 1], (seqs, key_dim))
    scales[:, :LANES] = jnp.broadcast_to(row_scale, weights.shape)
    scales[:, LANES:] = jnp.broadcast_to(weights[:, :1], weights.shape)

    def query_wait(t):
        arrived(qbuf.at[pl.ds(0, levels - 1), pl.ds(0, GROUP)], q_recv.at[t])

    def own_and_gate(last):
        rest, squares = restbuf[...], sqbuf[...]
        arrived(kx.at[pl.ds(0, levels - 1), pl.ds(0, heads - 1)], k2_recv)
        for l in peers:
            more = piece(l, lambda h: kx[l, h])
            rest, squares = rest + more[0], squares + more[1]
        rest = rest * lax.rsqrt(jnp.sum(squares, axis=1, keepdims=True) / width + 1e-06)
        key, value, gate = [rest[:, j * key_dim : (j + 1) * key_dim] for j in range(3)]
        gates[mine, :] = gate * jax.nn.sigmoid(gate)
        for peer in peers:
            send(gates.at[mine], gates.at[mine], sent, g_recv.at[me_l], (me_h, peer))
        if last:
            query_wait(groups - 1)
        query = qbuf[0, own_rows, :]
        for l in range(1, levels):
            query += qbuf[l, own_rows, :]
        query = query * scales[mine, :LANES]
        own = jnp.sum(query * key, axis=1, keepdims=True) * key_dim ** (-0.5) * value
        ownbuf[...] = scales[mine, LANES:] * own

    def own_send():
        mbuf[me_l, own_rows, :] += ownbuf[...]
        reads_send(my_t)

    seq_in = lax.broadcasted_iota(jnp.int32, (GROUP, val_dim), 0)
    def reads_send(t):
        part = mbuf.at[me_l, pl.ds(pl.multiple_of(t * GROUP, GROUP), GROUP)]
        for peer in peers:
            send(part, part, sent, m_recv.at[t], (me_h, peer))

    def read_group(t, n):
        here = pl.ds(t * GROUP, GROUP)
        reads = jnp.zeros((GROUP, val_dim), f32)
        if n:
            query = qbuf[0, here, :]
            for l in range(1, levels):
                query += qbuf[l, here, :]
            low = (query * rows_of_group(scales, t)).astype(bf16).astype(f32)
            left = jnp.concatenate(
                [(low * rows_of_group(wexp, t, j * key_dim, (j + 1) * key_dim)).astype(bf16) for j in range(n)], axis=1)
            for i in range(GROUP):
                seq = order[t] * GROUP + i
                got = jnp.dot(left, sbuf[seq, : n * key_dim, :], preferred_element_type=f32)
                reads = jnp.where(seq_in == i, got, reads)
        mbuf[me_l, here, :] = reads

        @pl.when(order[t] != my_block)
        def _():
            reads_send(t)

    for n in counts:
        @pl.when(count == n)
        def _():
            if n:
                arrived(sbuf.at[:, pl.ds(0, n * key_dim)], s_sem)
            for t in range(groups - 1):
                query_wait(t)
                read_group(t, n)
            if n < level_here:
                query_wait(groups - 1)
                read_group(groups - 1, n)
            own_and_gate(n == level_here)
            if n < level_here:
                own_send()
            else:
                pl.when(my_t < groups - 1)(own_send)
                read_group(groups - 1, n)
                pl.when(my_t == groups - 1)(own_send)

    def nearest(l, own, s):
        return sorted(range(groups), key=lambda b: (b == own, abs((2 * b + 1) * levels - (2 * l + 1) * groups), b))[s]

    ow_copy.wait()
    for s in range(groups):
        b = by_level(lambda l: nearest(l, 0, s))
        for own in range(1, groups):
            b = jnp.where(block == own, by_level(lambda l: nearest(l, own, s)), b)
        t = groups - 1 - exclusive_or(block, b, groups)
        for o in range(GROUP // owned):
            owner = b * (GROUP // owned) + o

            @pl.when(owner != me_l)
            def _():
                arrived(gates.at[pl.ds(0, owned)], g_recv.at[owner])

        arrived(mbuf.at[pl.ds(0, levels - 1), pl.ds(0, GROUP)], m_recv.at[t])
        here = pl.ds(pl.multiple_of(t * GROUP, GROUP), GROUP)
        rows = pl.ds(pl.multiple_of(b * GROUP, GROUP), GROUP)
        gated = mbuf[0, here, :]
        for l in range(1, levels):
            gated += mbuf[l, here, :]
        gated = gated * gates[rows, :]
        total_sq = jnp.broadcast_to(jnp.sum(gated * gated, axis=1, keepdims=True), (GROUP, LANES))
        product = jnp.dot((gated * ogain[...]).astype(bf16), owbuf[...], preferred_element_type=f32)
        for j in range(per):
            osend[b, j, :, :out_cols] = product[j * out_rows : (j + 1) * out_rows]
            osend[b, j, :, out_cols:] = total_sq[j * out_rows : (j + 1) * out_rows]
        for j in range(per):
            @pl.when(b * per + j != me_h)
            def _():
                send(osend.at[b, j], orecv.at[me_h], sent, o_recv, (b * per + j, me_l))

    total = osend[block, me_j]
    arrived(orecv.at[pl.ds(0, heads - 1)], o_recv)
    for o in range(1, heads):
        total += orecv[lax.rem(me_h + heads - o, heads)]
    mean = total[:, out_cols : out_cols + 1] / (heads * val_dim)
    out[...] = total[:, :out_cols] * lax.rsqrt(mean + 1e-05)
    arrived(xbuf.at[pl.ds(0, heads - 1)], sent)
    arrived(kx.at[pl.ds(0, levels - 1), 0], sent)
    arrived(kx.at[pl.ds(0, levels - 1), pl.ds(0, heads - 1)], sent)
    arrived(tbuf.at[pl.ds(0, levels - 1)], sent)
    arrived(qbuf.at[pl.ds(0, levels - 1)], sent)
    arrived(gates.at[pl.ds(0, seqs - owned)], sent)
    arrived(mbuf.at[pl.ds(0, levels - 1)], sent)
    arrived(orecv.at[pl.ds(0, heads - 1)], sent)


def body(features, in_gain, in_weight, level_bias, states, positions, out_gain, out_weight):
    heads, levels = lax.axis_size("head"), lax.axis_size("level")
    seqs, fw = features.shape
    width, cols = in_weight.shape
    _, head_here, level_here, key_dim, val_dim = states.shape
    level_total = level_bias.shape[1]
    assert seqs // levels <= GROUP and head_here == 1 and key_dim == LANES and val_dim == LANES
    out_cols = out_weight.shape[1]
    flipped = fw % LANES == 0
    slots = LANES // (1 << level_total.bit_length())
    owned, out_rows, groups = seqs // levels, seqs // heads, seqs // GROUP
    f32, bf16 = jnp.float32, jnp.bfloat16
    vmem, anyspace = pl.BlockSpec(memory_space=pltpu.VMEM), pl.BlockSpec(memory_space=pl.ANY)
    dma = pltpu.SemaphoreType.DMA
    return pl.pallas_call(
        functools.partial(kernel, heads, levels, in_gain.shape[0], (key_dim, val_dim, level_total, level_here)),
        out_shape=pltpu.VMEM((out_rows, out_cols), f32),
        in_specs=[anyspace] * 8,
        out_specs=vmem,
        scratch_shapes=[
            pltpu.VMEM((heads * levels, fw), f32),
            pltpu.VMEM(level_bias.shape, f32),
            pltpu.VMEM((1, seqs), jnp.int32),
            pltpu.VMEM((1, val_dim), f32),
            pltpu.VMEM((heads, seqs, fw), f32),
            pltpu.VMEM((cols, width) if flipped else (width, cols), bf16),
            pltpu.VMEM((seqs, level_here * key_dim, val_dim), bf16),
            pltpu.VMEM(out_weight.shape, bf16),
            pltpu.VMEM((seqs, LANES), f32),
            pltpu.VMEM((levels, seqs // slots, LANES), f32),
            pltpu.VMEM((levels, seqs, key_dim), f32),
            pltpu.VMEM((seqs, key_dim), f32),
            pltpu.VMEM((levels, heads, owned, fw), f32),
            pltpu.VMEM((seqs, val_dim), f32),
            pltpu.VMEM((owned, 3 * LANES), f32),
            pltpu.VMEM((owned, fw), f32),
            pltpu.VMEM((owned, val_dim), f32),
            pltpu.VMEM((seqs, level_here * key_dim), f32),
            pltpu.VMEM((seqs, 2 * LANES), f32),
            pltpu.VMEM((levels, seqs, val_dim), f32),
            pltpu.VMEM((groups, heads // groups, out_rows, out_cols + LANES), f32),
            pltpu.VMEM((heads, out_rows, out_cols + LANES), f32),
            pltpu.VMEM((1, LANES), f32),
            pltpu.SemaphoreType.REGULAR,
            dma((4,)), *[dma(())] * 5, dma((heads,)), dma((levels,)), dma(()),
            dma(()), dma((groups,)), dma((levels,)), dma((groups,)), dma(()),
        ],
        compiler_params=pltpu.CompilerParams(collective_id=0, has_side_effects=True),
    )(
        features,
        in_gain.reshape(heads * levels, fw),
        in_weight.T if flipped else in_weight,
        level_bias,
        states.reshape(seqs, level_here * key_dim, val_dim),
        positions.reshape(1, seqs),
        out_gain.reshape(1, val_dim),
        out_weight,
    )


def solution(mesh):
    in_specs = (
        P(None, ("head", "level")),
        P(),
        P(None, "head"),
        P("head", None),
        P(None, "head", "level", None, None),
        P(),
        P("head"),
        P("head", "level"),
    )
    out_specs = P("head", "level")
    return jax.shard_map(body, mesh=mesh, in_specs=in_specs, out_specs=out_specs, check_vma=False)
```

time: 25.8 us -> 25 us (0.969)
  Pallas kernels: 25.1 us -> 24.3 us
    pallas_call x1, Pallas kernels: 25.1 us -> 24.3 us  [body(): pl.pallas_call(functools.partial(kernel, heads, levels, in_gain.shape[0],...]
where the time goes in v3:
time: 25 us; the launch traced here: 24.9 us
  Pallas kernels  24.3 us (97%)
  local copies, waits for them, and re-layouts  0.62 us (2%)
    pallas_call x1, Pallas kernels, body(): pl.pallas_call(functools.partial(kernel, heads, levels, in_gain.shape[0],...  24.3 us
    unnamed x1, local copies, waits for them, and re-layouts  0.62 us

profile of v3, /device:TPU:0, one launch (start us, length us, event | category | flops | bytes accessed | tf_op | source)
XLA Modules:
  0.0 24.9 jit_solution(8372929075685662449)
XLA Ops:
  0.0 24.3 %shard_map.82 = f32[8,1024]{1,0:T(8,128)S(1)} custom-call(f32[64,128]{1,0:T(8,128)} %feat.1, f32[32,128]{1,0:T(8,128)} %bitcast.7, bf16[536,4096]{1,0:T(8,128)(2,1)} %bitcast.6, f32[1,24]{1,0:T(1,128)} %bias_any.1, bf16[64,768,128]{2,1,0:T(8,128)(2,1)} %bitcast.5, s32[1,64]{1,0:T(1,128)} %bitcast.8, f32[1,128]{1,0:T(1,128)} %bitcast.9, bf16[128,1024]{1,0:T(8,128)(2,1)} %outw.1), custom_call_target="tpu_custom_call" | custom-call | tf_op jit(solution)/shard_map/pallas_call | solution.py:393
  24.3 0.6 %copy.10 = f32[8,1024]{1,0:T(8,128)} copy(f32[8,1024]{1,0:T(8,128)S(1)} %shard_map.82) | data formatting | bytes 65536

commit v4 on v3

--- a/solution.py
+++ b/solution.py
@@ -40,9 +40,9 @@
     heads, levels, width, dims,
     feat, gain_any, inw, bias_any, states, pos_any, ogain_any, outw, out,
     gain, bias, pos, ogain, xbuf, wbuf, sbuf, owbuf, tailbuf, tbuf, qbuf, qtmp, kx, gates, restbuf, sqbuf, ownbuf,
-    wexp, scales, mbuf, osend, orecv, biasbuf,
-    z_sem, small_sem, x_sem, w_sem, s_sem, ow_sem, sent, f_recv, kx_recv, k2_recv,
-    t_recv, q_recv, g_recv, m_recv, o_recv,
+    wexp, scales, mbuf, osend, orecv, qsend, qrow, biasbuf,
+    z_sem, x_sem, w_sem, s_sem, ow_sem, sent, f_recv, kx_recv, k2_recv,
+    t_recv, q_recv, g_recv, m_recv, o_recv, r_recv,
 ):
     key_dim, val_dim, level_total, level_here = dims
     seqs, fw = feat.shape
@@ -62,7 +62,6 @@
     my_t = groups - 1 - exclusive_or(block, my_block, groups)
     own_rows = pl.ds(pl.multiple_of(my_t * GROUP + lax.rem(me_l * owned, GROUP), owned), owned)
     mine = pl.ds(pl.multiple_of(me_l * owned, owned), owned)
-    peers = [l + jnp.where(me_l <= l, 1, 0) for l in range(levels - 1)]
 
     def by_level(choice):
         value = jnp.int32(choice(0))
@@ -70,6 +69,9 @@
             value = jnp.where(me_l == l, choice(l), value)
         return value
 
+    peers = [
+        by_level(lambda me: sorted((p for p in range(levels) if p != me), key=lambda p: (-abs(p - me), p))[s])
+        for s in range(levels - 1)]
     tail0 = 2 * key_dim + 2 * val_dim
     f32, bf16 = jnp.float32, jnp.bfloat16
 
@@ -92,8 +94,8 @@
     for o in range(1, heads):
         tell(barrier, lax.rem(me_h + o, heads), me_l)
     smalls = [
-        pltpu.make_async_copy(a, b, small_sem.at[i])
-        for i, (a, b) in enumerate(((gain_any, gain), (bias_any, bias), (pos_any, pos), (ogain_any, ogain)))]
+        pltpu.make_async_copy(a, b, w_sem)
+        for a, b in ((gain_any, gain), (bias_any, bias), (pos_any, pos), (ogain_any, ogain))]
     for c in smalls:
         c.start()
     if flipped:
@@ -132,6 +134,20 @@
         send(xbuf.at[me_h, theirs], kx.at[me_l, me_h], sent, kx_recv.at[me_l], (me_h, l))
 
     pl.loop(0, me_l)(rows_send)
+    possible = min(level_total, POSITION_BITS + 1)
+    counts = sorted({min(max(possible - l * level_here, 0), level_here) for l in range(levels)})
+    count = jnp.clip(possible - me_l * level_here, 0, level_here)
+
+    def state_start(t, n):
+        part = (group_rows(t), pl.ds(0, n * key_dim))
+        pltpu.make_async_copy(states.at[part], sbuf.at[part], s_sem).start()
+
+    for n in counts:
+        @pl.when(jnp.logical_and(count == n, n > 0))
+        def _():
+            for t in range(groups):
+                state_start(t, n)
+
     for c in smalls:
         c.wait()
     arrived(wbuf, w_sem)
@@ -185,20 +201,6 @@
         for peer in peers:
             send(part, part, sent, q_recv.at[t], (me_h, peer))
 
-    possible = min(level_total, POSITION_BITS + 1)
-    counts = sorted({min(max(possible - l * level_here, 0), level_here) for l in range(levels)})
-    count = jnp.clip(possible - me_l * level_here, 0, level_here)
-
-    def state_start(t, n):
-        part = (group_rows(t), pl.ds(0, n * key_dim))
-        pltpu.make_async_copy(states.at[part], sbuf.at[part], s_sem).start()
-
-    for n in counts:
-        @pl.when(jnp.logical_and(count == n, n > 0))
-        def _():
-            for t in range(groups):
-                state_start(t, n)
-
     ow_copy = pltpu.make_async_copy(outw, owbuf, ow_sem)
     ow_copy.start()
 
@@ -230,13 +232,14 @@
 
         return lax.fori_loop(0, heads, step, (jnp.zeros((owned, tail0 - key_dim), f32), total))
 
-    restbuf[...], sqbuf[...] = piece(me_l, lambda h: xbuf[h, mine, :])
     for s in range(levels - 1):
         l = by_level(lambda me: sorted((p for p in range(levels) if p != me), key=lambda p: (abs(p - me), p))[s])
         arrived(kx.at[0, 0], kx_recv.at[l])
         part = kx.at[l, me_h]
         for target in [mirror, 2 * mirror_chip + 1 - core] + direct + [buddy]:
             send(part, part, sent, k2_recv, (target, me_l))
+
+    restbuf[...], sqbuf[...] = piece(me_l, lambda h: xbuf[h, mine, :])
 
     arrived(tbuf.at[pl.ds(0, levels - 1)], t_recv)
     pack = tbuf[0]
@@ -331,6 +334,8 @@
         return sorted(range(groups), key=lambda b: (b == own, abs((2 * b + 1) * levels - (2 * l + 1) * groups), b))[s]
 
     ow_copy.wait()
+    lane_of = lax.broadcasted_iota(jnp.int32, (GROUP, LANES), 1)
+    row_of = lax.broadcasted_iota(jnp.int32, (GROUP, LANES), 0)
     for s in range(groups):
         b = by_level(lambda l: nearest(l, 0, s))
         for own in range(1, groups):
@@ -351,21 +356,29 @@
             gated += mbuf[l, here, :]
         gated = gated * gates[rows, :]
         total_sq = jnp.broadcast_to(jnp.sum(gated * gated, axis=1, keepdims=True), (GROUP, LANES))
+        qsend[b] = jnp.sum(jnp.where(row_of == lane_of, total_sq, 0.0), axis=0, keepdims=True)
         product = jnp.dot((gated * ogain[...]).astype(bf16), owbuf[...], preferred_element_type=f32)
         for j in range(per):
-            osend[b, j, :, :out_cols] = product[j * out_rows : (j + 1) * out_rows]
-            osend[b, j, :, out_cols:] = total_sq[j * out_rows : (j + 1) * out_rows]
+            osend[b, j] = product[j * out_rows : (j + 1) * out_rows]
         for j in range(per):
             @pl.when(b * per + j != me_h)
             def _():
+                send(qsend.at[b], qrow.at[me_h], sent, r_recv, (b * per + j, me_l))
                 send(osend.at[b, j], orecv.at[me_h], sent, o_recv, (b * per + j, me_l))
 
     total = osend[block, me_j]
+    square = qsend[block]
+    arrived(qrow.at[pl.ds(0, heads - 1)], r_recv)
+    for o in range(1, heads):
+        square += qrow[lax.rem(me_h + heads - o, heads)]
+    lane_of = lax.broadcasted_iota(jnp.int32, (out_rows, LANES), 1)
+    row_of = lax.broadcasted_iota(jnp.int32, (out_rows, LANES), 0) + me_j * out_rows
+    square = jnp.where(row_of == lane_of, jnp.broadcast_to(square, (out_rows, LANES)), 0.0)
+    factor = lax.rsqrt(jnp.sum(square, axis=1, keepdims=True) / (heads * val_dim) + 1e-05)
     arrived(orecv.at[pl.ds(0, heads - 1)], o_recv)
     for o in range(1, heads):
         total += orecv[lax.rem(me_h + heads - o, heads)]
-    mean = total[:, out_cols : out_cols + 1] / (heads * val_dim)
-    out[...] = total[:, :out_cols] * lax.rsqrt(mean + 1e-05)
+    out[...] = total * factor
     arrived(xbuf.at[pl.ds(0, heads - 1)], sent)
     arrived(kx.at[pl.ds(0, levels - 1), 0], sent)
     arrived(kx.at[pl.ds(0, levels - 1), pl.ds(0, heads - 1)], sent)
@@ -374,6 +387,7 @@
     arrived(gates.at[pl.ds(0, seqs - owned)], sent)
     arrived(mbuf.at[pl.ds(0, levels - 1)], sent)
     arrived(orecv.at[pl.ds(0, heads - 1)], sent)
+    arrived(qrow.at[pl.ds(0, heads - 1)], sent)
 
 
 def body(features, in_gain, in_weight, level_bias, states, positions, out_gain, out_weight):
@@ -416,12 +430,14 @@
             pltpu.VMEM((seqs, level_here * key_dim), f32),
             pltpu.VMEM((seqs, 2 * LANES), f32),
             pltpu.VMEM((levels, seqs, val_dim), f32),
-            pltpu.VMEM((groups, heads // groups, out_rows, out_cols + LANES), f32),
-            pltpu.VMEM((heads, out_rows, out_cols + LANES), f32),
+            pltpu.VMEM((groups, heads // groups, out_rows, out_cols), f32),
+            pltpu.VMEM((heads, out_rows, out_cols), f32),
+            pltpu.VMEM((groups, 1, LANES), f32),
+            pltpu.VMEM((heads, 1, LANES), f32),
             pltpu.VMEM((1, LANES), f32),
             pltpu.SemaphoreType.REGULAR,
-            dma((4,)), *[dma(())] * 5, dma((heads,)), dma((levels,)), dma(()),
-            dma(()), dma((groups,)), dma((levels,)), dma((groups,)), dma(()),
+            *[dma(())] * 5, dma((heads,)), dma((levels,)), dma(()),
+            dma(()), dma((groups,)), dma((levels,)), dma((groups,)), dma(()), dma(()),
         ],
         compiler_params=pltpu.CompilerParams(collective_id=0, has_side_effects=True),
     )(

time: 25 us -> 23.4 us (0.936)
  Pallas kernels: 24.3 us -> 22.6 us
    pallas_call x1, Pallas kernels: 24.3 us -> 22.6 us  [body(): pl.pallas_call(functools.partial(kernel, heads, levels, in_gain.shape[0],...]
where the time goes in v4:
time: 23.4 us; the launch traced here: 23.3 us
  Pallas kernels  22.6 us (97%)
  local copies, waits for them, and re-layouts  0.62 us (3%)
    pallas_call x1, Pallas kernels, body(): pl.pallas_call(functools.partial(kernel, heads, levels, in_gain.shape[0],...  22.6 us
    unnamed x1, local copies, waits for them, and re-layouts  0.62 us

profile of v4, /device:TPU:0, one launch (start us, length us, event | category | flops | bytes accessed | tf_op | source)
XLA Modules:
  0.0 23.3 jit_solution(4573742849247773557)
XLA Ops:
  0.0 22.6 %shard_map.82 = f32[8,1024]{1,0:T(8,128)S(1)} custom-call(f32[64,128]{1,0:T(8,128)} %feat.1, f32[32,128]{1,0:T(8,128)} %bitcast.7, bf16[536,4096]{1,0:T(8,128)(2,1)} %bitcast.6, f32[1,24]{1,0:T(1,128)} %bias_any.1, bf16[64,768,128]{2,1,0:T(8,128)(2,1)} %bitcast.5, s32[1,64]{1,0:T(1,128)} %bitcast.8, f32[1,128]{1,0:T(1,128)} %bitcast.9, bf16[128,1024]{1,0:T(8,128)(2,1)} %outw.1), custom_call_target="tpu_custom_call" | custom-call | tf_op jit(solution)/shard_map/pallas_call | solution.py:407
  22.6 0.6 %copy.10 = f32[8,1024]{1,0:T(8,128)} copy(f32[8,1024]{1,0:T(8,128)S(1)} %shard_map.82) | data formatting | bytes 65536

commit v5 on v4

--- a/solution.py
+++ b/solution.py
@@ -131,7 +131,7 @@
 
     def rows_send(l):
         theirs = pl.ds(pl.multiple_of(l * owned, owned), owned)
-        send(xbuf.at[me_h, theirs], kx.at[me_l, me_h], sent, kx_recv.at[me_l], (me_h, l))
+        send(xbuf.at[me_h, theirs], kx.at[me_l, me_h], sent, kx_recv, (me_h, l))
 
     pl.loop(0, me_l)(rows_send)
     possible = min(level_total, POSITION_BITS + 1)
@@ -170,7 +170,7 @@
             def _():
                 pl.semaphore_wait(z_sem, levels - 1 - me_l)
 
-            pl.loop(me_l + 1, levels)(rows_send)
+            pl.loop(0, levels - 1 - me_l)(lambda s: rows_send(levels - 1 - s))
         if i:
             feature_wait(src)
         if i == 2:
@@ -232,9 +232,8 @@
 
         return lax.fori_loop(0, heads, step, (jnp.zeros((owned, tail0 - key_dim), f32), total))
 
-    for s in range(levels - 1):
-        l = by_level(lambda me: sorted((p for p in range(levels) if p != me), key=lambda p: (abs(p - me), p))[s])
-        arrived(kx.at[0, 0], kx_recv.at[l])
+    arrived(kx.at[pl.ds(0, levels - 1), 0], kx_recv)
+    for l in peers:
         part = kx.at[l, me_h]
         for target in [mirror, 2 * mirror_chip + 1 - core] + direct + [buddy]:
             send(part, part, sent, k2_recv, (target, me_l))
@@ -436,7 +435,7 @@
             pltpu.VMEM((heads, 1, LANES), f32),
             pltpu.VMEM((1, LANES), f32),
             pltpu.SemaphoreType.REGULAR,
-            *[dma(())] * 5, dma((heads,)), dma((levels,)), dma(()),
+            *[dma(())] * 5, dma((heads,)), dma(()), dma(()),
             dma(()), dma((groups,)), dma((levels,)), dma((groups,)), dma(()), dma(()),
         ],
         compiler_params=pltpu.CompilerParams(collective_id=0, has_side_effects=True),

time: 23.4 us -> 23.3 us (level)
    pallas_call x1, Pallas kernels: 22.6 us -> 22.4 us  [body(): pl.pallas_call(functools.partial(kernel, heads, levels, in_gain.shape[0],...]
where the time goes in v5:
time: 23.3 us; the launch traced here: 23 us
  Pallas kernels  22.4 us (96%)
  local copies, waits for them, and re-layouts  0.62 us (3%)
    pallas_call x1, Pallas kernels, body(): pl.pallas_call(functools.partial(kernel, heads, levels, in_gain.shape[0],...  22.4 us
    unnamed x1, local copies, waits for them, and re-layouts  0.62 us

profile of v5, /device:TPU:0, one launch (start us, length us, event | category | flops | bytes accessed | tf_op | source)
XLA Modules:
  0.0 23.0 jit_solution(14318147723816547896)
XLA Ops:
  0.0 22.4 %shard_map.82 = f32[8,1024]{1,0:T(8,128)S(1)} custom-call(f32[64,128]{1,0:T(8,128)} %feat.1, f32[32,128]{1,0:T(8,128)} %bitcast.7, bf16[536,4096]{1,0:T(8,128)(2,1)} %bitcast.6, f32[1,24]{1,0:T(1,128)} %bias_any.1, bf16[64,768,128]{2,1,0:T(8,128)(2,1)} %bitcast.5, s32[1,64]{1,0:T(1,128)} %bitcast.8, f32[1,128]{1,0:T(1,128)} %bitcast.9, bf16[128,1024]{1,0:T(8,128)(2,1)} %outw.1), custom_call_target="tpu_custom_call" | custom-call | tf_op jit(solution)/shard_map/pallas_call | solution.py:406
  22.4 0.6 %copy.10 = f32[8,1024]{1,0:T(8,128)} copy(f32[8,1024]{1,0:T(8,128)S(1)} %shard_map.82) | data formatting | bytes 65536
